TPU v7x, 32 devices: a whole 2x2x4 slice. The times are simulated.
32 devices in a mesh: replica: 2 (over x), fsdp: 16 (over z, y, core).
Axes of the slice: x: 2, y: 2, z: 4, core: 2. Of those that a mesh axis runs over, the one named last changes fastest.
Arguments:
- act: bfloat16 [2, 2, 6144, 2048], P('replica', None, 'fsdp'), may hold values from -6 to 6
- target: bfloat16 [2, 2, 6144, 512], P('replica', None, 'fsdp'), may hold values from -6 to 6
- weights: float32 [2, 2048, 512], P('replica', 'fsdp'), may hold values from -6 to 6
- inner_m: float32 [2, 2048, 512], P('replica', 'fsdp'), may hold values from -0.0006 to 0.0006
- inner_v: float32 [2, 2048, 512], P('replica', 'fsdp'), may hold values from 2e-09 to 2e-08
- outer_delta: float32 [2, 2048, 512], P('replica', 'fsdp'), may hold values from -4 to 4
- anchor: float32 [2048, 512], P('fsdp'), may hold values from -6 to 6
- outer_mom: float32 [2048, 512], P('fsdp'), may hold values from -1.5 to 1.5
Outputs:
- new_weights: float32 [2, 2048, 512], P('replica', 'fsdp')
- new_m: float32 [2, 2048, 512], P('replica', 'fsdp')
- new_v: float32 [2, 2048, 512], P('replica', 'fsdp')
- new_anchor: float32 [2048, 512], P('fsdp')
- new_mom: float32 [2048, 512], P('fsdp')
All inputs are finite; a program needn't handle non-finite values.
Results may differ from a plain program's by a relative error of at most 0.0034.
Values may be sent and summed in bfloat16 or wider, within the bound.
A program may use at most 64 MiB of HBM per device.

v0:
```python
import jax
import jax.numpy as jnp
from jax import lax
from jax.sharding import PartitionSpec as P


def add_rows(piece, inputs):
    return jnp.dot(inputs, piece, preferred_element_type=jnp.float32)


def body(act, target, weights, inner_m, inner_v, outer_delta, anchor, outer_mom):
    micro_count = act.shape[1]
    tok_rows = act.shape[2]
    feat_count = act.shape[3]
    in_scale = feat_count ** (-0.5)
    shard_low = weights[0].astype(jnp.bfloat16)
    out_width = shard_low.shape[1]
    flat_act = act[0].reshape(micro_count * tok_rows, feat_count)
    results = []
    for micro_id in range(micro_count):
        inputs = act[0, micro_id]

        def fold_one(running, piece, start, inputs=inputs):
            return add_rows(piece, inputs)

        empty = jnp.zeros((tok_rows, out_width), jnp.float32)
        results.append(
            fold_one(empty, lax.all_gather(shard_low, "fsdp", axis=0, tiled=True), jnp.int32(0))
        )
    summed = jnp.concatenate(results, axis=0)
    predicted = summed * in_scale
    wanted = target[0].reshape(micro_count * tok_rows, out_width).astype(jnp.float32)
    resid = (predicted - wanted).astype(jnp.bfloat16)
    grad_rows = lax.psum_scatter(
        lax.dot_general(
            flat_act, resid, (((0,), (0,)), ((), ())), preferred_element_type=jnp.float32
        ),
        "fsdp",
        scatter_dimension=0,
        tiled=True,
    )
    grad = grad_rows * (in_scale / (micro_count * tok_rows * lax.axis_size("fsdp")))
    moment = 0.9 * inner_m[0] + 0.1 * grad
    second = 0.95 * inner_v[0] + 0.05 * grad * grad
    trained = weights[0] - 0.3 * moment / (jnp.sqrt(second) + 1e-08)
    groups = lax.axis_size("replica")
    block_width = out_width // groups
    blocks = lax.all_to_all(outer_delta, "replica", split_axis=2, concat_axis=0, tiled=True)
    mean_part = jnp.sum(blocks, axis=0) / groups
    offset = lax.axis_index("replica") * block_width
    mom_part = lax.dynamic_slice_in_dim(outer_mom, offset, block_width, 1)
    anchor_part = lax.dynamic_slice_in_dim(anchor, offset, block_width, 1)
    mom_next = 0.9 * mom_part + mean_part
    anchor_next = anchor_part - 0.7 * (mean_part + 0.9 * mom_next)
    new_anchor, new_mom = (
        lax.all_gather(anchor_next, "replica", axis=1, tiled=True),
        lax.all_gather(mom_next, "replica", axis=1, tiled=True),
    )
    mixed = 0.5 * trained + 0.5 * new_anchor
    return (mixed[None], moment[None], second[None], new_anchor, new_mom)


def solution(mesh):
    in_specs = (
        P("replica", None, "fsdp", None),
        P("replica", None, "fsdp", None),
        P("replica", "fsdp", None),
        P("replica", "fsdp", None),
        P("replica", "fsdp", None),
        P("replica", "fsdp", None),
        P("fsdp", None),
        P("fsdp", None),
    )
    out_specs = (
        P("replica", "fsdp", None),
        P("replica", "fsdp", None),
        P("replica", "fsdp", None),
        P("fsdp", None),
        P("fsdp", None),
    )
    return jax.shard_map(body, mesh=mesh, in_specs=in_specs, out_specs=out_specs, check_vma=False)
```

profile of v0, /device:TPU:0, one launch (start us, length us, event | category | flops | bytes accessed | tf_op | source)
XLA Modules:
  0.0 146.3 jit_solution(11024401022935197334)
XLA Ops:
  7.2 0.0 all-gather.2.cloned.1.call-start
  7.2 1.1 copy.24
  8.3 0.7 bitcast_convert_fusion
  9.0 0.0 all-gather.2.cloned.1.call-update
  9.0 0.0 copy-start
  9.0 0.0 reduce-scatter.2.cloned.1.call-start
  9.1 45.4 %all-gather.2.cloned.1.call-done = bf16[2048,512]{0,1:T(8,128)(2,1)} async-done(((bf16[128,512]{0,1:T(8,128)(2,1)}), bf16[2048,512]{0,1:T(8,128)(2,1)}) %all-gather.2.cloned.1.call-update) | async-done | bytes 2097168 | tf_op jit(solution)/shard_map/all_gather | solution.py:28
  54.5 0.0 copy-start.7
  54.5 3.2 %fusion.1 = f32[384,512]{1,0:T(8,128)S(1)} fusion(bf16[2048,512]{0,1:T(8,128)(2,1)} %all-gather.2.cloned.1.call-done, bf16[1,2,384,2048]{3,2,1,0:T(8,128)(2,1)} %param.8), kind=kOutput, calls=%fused_computation.3 | convolution fusion | flops 805306368 | bytes 4456448 | tf_op jit(solution)/shard_map/dot_general | solution.py:8
  57.7 0.0 copy-done
  57.7 0.0 copy-done.7
  57.7 1.0 fusion.3
  58.8 0.0 copy-start.1
  58.8 0.2 maximum_multiply_fusion
  59.0 0.9 copy-done.1
  59.9 3.8 %convolution_bitcast_fusion = f32[2048,512]{0,1:T(8,128)} fusion(bf16[1,2,384,2048]{3,2,1,0:T(8,128)(2,1)S(1)} %copy-done, f32[1,2,384,512]{3,2,1,0:T(8,128)S(1)} %bitcast.47, bf16[1,2,384,512]{3,2,1,0:T(8,128)(2,1)S(1)} %copy-done.1), kind=kOutput, calls=%fused_computation | convolution fusion | flops 1611792384 | bytes 9699328 | tf_op jit(solution)/shard_map/dot_general | solution.py:35
  63.8 0.0 copy-start.2
  63.8 0.0 copy-start.3
  63.8 0.0 copy-start.5
  63.8 0.0 copy-start.6
  63.8 0.0 reduce-scatter.2.cloned.1.call-update
  63.8 0.9 copy-done.2
  64.7 0.0 copy-start.4
  64.7 0.8 copy.29
  65.6 3.5 %all-to-all-start = ((f32[1,128,512]{1,0,2:T(1,128)}), f32[1,128,512]{1,0,2:T(1,128)S(1)}, u32[]{:S(2)}, u32[]{:S(2)}) async-start(f32[1,128,512]{1,0,2:T(1,128)} %copy.29), calls=%async_computation.1 | async-start | bytes 524288 | tf_op jit(solution)/shard_map/all_to_all | solution.py:48
  69.0 0.0 copy-done.3
  69.0 0.1 copy.27
  69.2 0.0 copy-done.5
  69.2 0.0 copy-done.6
  69.2 0.1 copy.41
  69.3 0.1 copy.40
  69.4 0.0 copy-done.4
  69.4 0.1 copy.25
  69.5 5.3 %all-to-all-done = f32[1,128,512]{1,0,2:T(1,128)S(1)} async-done(((f32[1,128,512]{1,0,2:T(1,128)}), f32[1,128,512]{1,0,2:T(1,128)S(1)}, u32[]{:S(2)}, u32[]{:S(2)}) %all-to-all-start) | async-done | bytes 262176 | tf_op jit(solution)/shard_map/all_to_all | solution.py:48
  74.9 5.6 %all_gather.11 = f32[128,512]{0,1:T(8,128)S(1)} all-gather(f32[128,256]{0,1:T(8,128)S(1)} %get-tuple-element.19), channel_id=1, replica_groups=mesh['replica'=2,'fsdp'=16] {'replica'}, dimensions={1}, use_global_device_ids=true | all-gather | bytes 393216 | tf_op jit(solution)/shard_map/all_gather | solution.py:56
  80.5 0.8 copy.36
  81.4 5.6 %all_gather.12 = f32[128,512]{0,1:T(8,128)S(1)} all-gather(f32[128,256]{0,1:T(8,128)S(1)} %get-tuple-element.18), channel_id=1, replica_groups=mesh['replica'=2,'fsdp'=16] {'replica'}, dimensions={1}, use_global_device_ids=true | all-gather | bytes 393216 | tf_op jit(solution)/shard_map/all_gather | solution.py:57
  87.0 0.8 copy.37
  87.8 48.0 %reduce-scatter.2.cloned.1.call-done = f32[128,512]{0,1:T(8,128)} async-done(((f32[2048,512]{0,1:T(8,128)}), f32[128,512]{0,1:T(8,128)}) %reduce-scatter.2.cloned.1.call-update) | async-done | bytes 262160 | tf_op jit(solution)/shard_map/reduce_scatter | solution.py:34
  135.8 1.2 fusion.13
  137.0 0.8 copy.33
  137.8 0.8 copy.34
  138.7 0.8 copy.35
  (3 shorter events, 0.1 us)
Async XLA Ops:
  7.2 47.3 %all-gather.2.cloned.1.call-start = ((), (), s32[]{:S(2)}) async-start(), calls=%async_computation.2 | async-start | bytes 2228224 | tf_op jit(solution)/shard_map/all_gather | solution.py:28
  9.0 48.7 %copy-start = (bf16[1,2,384,2048]{3,2,1,0:T(8,128)(2,1)S(1)}, bf16[1,2,384,2048]{3,2,1,0:T(8,128)(2,1)}, u32[]{:S(2)}) copy-start(bf16[1,2,384,2048]{3,2,1,0:T(8,128)(2,1)} %param.8) | copy-start | bytes 9437188
  9.0 126.8 %reduce-scatter.2.cloned.1.call-start = ((), (), s32[]{:S(2)}) async-start(), calls=%async_computation.3 | async-start | bytes 4456448 | tf_op jit(solution)/shard_map/reduce_scatter | solution.py:34
  54.5 3.2 %copy-start.7 = (bf16[2048,512]{0,1:T(8,128)(2,1)S(1)}, bf16[2048,512]{0,1:T(8,128)(2,1)}, u32[]{:S(2)}) copy-start(bf16[2048,512]{0,1:T(8,128)(2,1)} %all-gather.2.cloned.1.call-done) | copy-start | bytes 6291460
  58.8 1.1 copy-start.1
  63.8 0.9 copy-start.2
  63.8 5.3 %copy-start.3 = (f32[1,128,512]{2,1,0:T(8,128)S(1)}, f32[1,128,512]{2,1,0:T(8,128)}, u32[]{:S(2)}) copy-start(f32[1,128,512]{2,1,0:T(8,128)} %param.12) | copy-start | bytes 786436
  63.8 5.4 %copy-start.5 = (f32[128,512]{1,0:T(8,128)S(1)}, f32[128,512]{1,0:T(8,128)}, u32[]{:S(2)}) copy-start(f32[128,512]{1,0:T(8,128)} %param.15) | copy-start | bytes 786436
  63.8 5.4 %copy-start.6 = (f32[128,512]{1,0:T(8,128)S(1)}, f32[128,512]{1,0:T(8,128)}, u32[]{:S(2)}) copy-start(f32[128,512]{1,0:T(8,128)} %param.14) | copy-start | bytes 786436
  64.7 4.7 %copy-start.4 = (f32[1,128,512]{2,1,0:T(8,128)S(1)}, f32[1,128,512]{2,1,0:T(8,128)}, u32[]{:S(2)}) copy-start(f32[1,128,512]{2,1,0:T(8,128)} %param.11) | copy-start | bytes 786436
  65.6 9.3 %all-to-all-start = ((f32[1,128,512]{1,0,2:T(1,128)}), f32[1,128,512]{1,0,2:T(1,128)S(1)}, u32[]{:S(2)}, u32[]{:S(2)}) async-start(f32[1,128,512]{1,0,2:T(1,128)} %copy.29), calls=%async_computation.1 | async-start | bytes 524288 | tf_op jit(solution)/shard_map/all_to_all | solution.py:48
Sparse Core Ops, SparseCore 0:
  10.7 43.7 all-gather.1
  63.9 71.8 reduce-scatter.1
where the time goes:
time: 147 us; the launch traced here: 146 us
  waiting for transfers between devices  98.8 us (67%)
  between operations  14.2 us (10%)
  blocking collectives  11.3 us (8%)
  local copies, waits for them, and re-layouts  8.42 us (6%)
  matrix products  8.09 us (6%)
  starting transfers between devices  3.53 us (2%)
  other arithmetic  2.06 us (1%)
    reduce_scatter x1, waiting for transfers between devices, body(): lax.psum_scatter(lax.dot_general(flat_act, resid, (((0,), (0,)), ((), ())...  48 us
    all_gather x1, waiting for transfers between devices, body(): lax.all_gather(shard_low, 'fsdp', axis=0, tiled=True)  45.4 us
    unnamed x27, local copies, waits for them, and re-layouts  8.39 us
    all_gather x1, blocking collectives, body(): lax.all_gather(anchor_next, 'replica', axis=1, tiled=True)  5.64 us
    all_gather x1, blocking collectives, body(): lax.all_gather(mom_next, 'replica', axis=1, tiled=True)  5.62 us
    all_to_all x1, waiting for transfers between devices, body(): lax.all_to_all(outer_delta, 'replica', split_axis=2, concat_axis=0, tiled...  5.3 us
    dot_general x2, matrix products, add_rows(): return jnp.dot(inputs, piece, preferred_element_type=jnp.float32)  4.26 us
    dot_general x1, matrix products, body(): lax.dot_general(flat_act, resid, (((0,), (0,)), ((), ())), preferred_elem...  3.83 us
  transfers between devices with their start and end apart: 3, of which 3 were waited for; matrix products, arithmetic and copies ran while one was open for 2% of the time, Pallas kernels for 0%

commit v1 on v0

v1 whole, which is shorter than its diff:
```python
import functools

import jax
import jax.numpy as jnp
from jax import lax
from jax.experimental import pallas as pl
from jax.experimental.pallas import tpu as pltpu
from jax.sharding import PartitionSpec as P

MESH = pl.DeviceIdType.MESH
PIECES = 2
LIMIT = 16


def flip(me, mask):
    out = me
    bit = 1
    while bit <= mask:
        if mask & bit:
            out = out + bit * (1 - 2 * ((me // bit) % 2))
        bit *= 2
    return out


def low(k):
    return k & -k


def arrivals(n):
    labels = [k for k in range(2, n, 2)]

    def when(k):
        return (bin(k).count("1"), -low(k)) if low(k) > 2 or k == 2 else (bin(k).count("1") + 1, -k)

    return sorted(labels, key=when)


def kernel(
    n, pieces, in_scale,
    act, target, weights, delta,
    grad_out, peer_out,
    wf, w, a, at, acc, tgt, res, g, sb, rb,
    w_sem, a_sem, t_sem, ag_send, ag_recv, rs_send, rs_recv, d_send, d_recv,
):
    me = lax.axis_index("fsdp")
    rep = lax.axis_index("replica")
    core = me % 2
    rows = weights.shape[0]
    part = rows // pieces
    pairs = n // 2
    width = 2 * rows
    tokens = act.shape[0]
    tile = 256 if tokens % 256 == 0 else tokens

    bits = [1 << j for j in range(n.bit_length() - 1)]

    w_copy = pltpu.make_async_copy(weights, wf, w_sem)
    w_copy.start()
    barrier = pltpu.get_barrier_semaphore()
    for b in bits:
        pl.semaphore_signal(barrier, inc=1, device_id=(rep, flip(me, b)), device_id_type=MESH)
    pl.semaphore_signal(barrier, inc=1, device_id=(1 - rep, me), device_id_type=MESH)
    a_copies = []
    for m in range(pairs):
        col = pl.multiple_of((flip(me, 2 * m) // 2) * width, width)
        a_copies.append(
            pltpu.make_async_copy(act.at[:, pl.ds(col, width)], a.at[m], a_sem.at[m])
        )
        a_copies[-1].start()
    t_copy = pltpu.make_async_copy(target, tgt, t_sem)
    t_copy.start()

    def spot(k, p):
        owner_core = core if k % 2 == 0 else 1 - core
        return pl.ds(pl.multiple_of(owner_core * rows + p * part, part), part)

    w_copy.wait()
    w[0, pl.ds(pl.multiple_of(core * rows, rows), rows), :] = wf[...].astype(jnp.bfloat16)
    pl.semaphore_wait(barrier, len(bits) + 1)

    def ag_copy(k, b, p):
        return pltpu.make_async_remote_copy(
            src_ref=w.at[k // 2, spot(k, p)],
            dst_ref=w.at[(k + b) // 2, spot(k, p)],
            send_sem=ag_send.at[k + b, p],
            recv_sem=ag_recv.at[k + b, p],
            device_id=(rep, flip(me, b)),
            device_id_type=MESH,
        )

    for b in reversed(bits):
        for p in range(pieces):
            ag_copy(0, b, p).start()
    d_copy = pltpu.make_async_remote_copy(
        src_ref=delta, dst_ref=peer_out, send_sem=d_send, recv_sem=d_recv,
        device_id=(1 - rep, me), device_id_type=MESH,
    )
    d_copy.start()

    turned = [False] * pairs

    def turn(m):
        if turned[m]:
            return
        turned[m] = True
        a_copies[m].wait()
        for t in range(0, tokens, tile):
            at[m, :, t : t + tile] = a[m, t : t + tile, :].T

    started = []

    def multiply(m):
        turn(m)
        first = not started
        started.append(m)

        @pl.loop(0, tokens // tile)
        def _(t):
            sl = pl.ds(pl.multiple_of(t * tile, tile), tile)
            prod = jnp.dot(a[m, sl, :], w[m], preferred_element_type=jnp.float32)
            if first:
                acc[sl, :] = prod
            else:
                acc[sl, :] += prod

    def got(k):
        b = low(k)
        for p in range(pieces):
            ag_copy(k - b, b, p).wait_recv()
            for c in reversed(bits):
                if c < b:
                    ag_copy(k, c, p).start()

    def finish(m):
        got(2 * m + 1)
        multiply(m)

    turn(0)
    finish(0)
    order = arrivals(n)
    pending = []
    for m, k in enumerate(order):
        turn(k // 2)
        got(k)
        if pending:
            finish(pending.pop(0))
        pending.append(k // 2)
    for m in pending:
        finish(m)

    t_copy.wait()

    @pl.loop(0, tokens // tile)
    def _(t):
        sl = pl.ds(pl.multiple_of(t * tile, tile), tile)
        res[sl, :] = (acc[sl, :] * in_scale - tgt[sl, :].astype(jnp.float32)).astype(jnp.bfloat16)

    mine = pl.ds(pl.multiple_of(core * rows, rows), rows)
    theirs = pl.ds(pl.multiple_of((1 - core) * rows, rows), rows)

    def rs_copy(k, p):
        b = low(k)
        where = pl.ds(p * part, part)
        if b == 1:
            where = pl.ds(0, rows)
        return pltpu.make_async_remote_copy(
            src_ref=sb.at[k, where],
            dst_ref=rb.at[k, where],
            send_sem=rs_send.at[k, p],
            recv_sem=rs_recv.at[k, p],
            device_id=(rep, flip(me, b)),
            device_id_type=MESH,
        )

    def produce(m):
        g[m] = jnp.dot(at[m], res[...], preferred_element_type=jnp.float32)
        sb[2 * m + 1] = g[m, theirs, :].astype(jnp.bfloat16)
        rs_copy(2 * m + 1, 0).start()

    def collect(k):
        b = low(k) if k else n
        rs_copy(k + 1, 0).wait_recv()
        base = pl.multiple_of(core * rows, rows)
        for p in range(pieces):
            total = g[k // 2, pl.ds(base + p * part, part), :] + rb[k + 1, p * part : (p + 1) * part, :].astype(jnp.float32)
            for c in bits[1:]:
                if c < b:
                    rs_copy(k + c, p).wait_recv()
                    total += rb[k + c, p * part : (p + 1) * part, :].astype(jnp.float32)
            if k:
                sb[k, p * part : (p + 1) * part, :] = total.astype(jnp.bfloat16)
                rs_copy(k, p).start()
            else:
                grad_out[p * part : (p + 1) * part, :] = total

    first = [k for k in range(n - 2, 0, -4)]
    rest = [k for k in range(n - 4, -1, -4)]
    waiting = []
    for k in first:
        produce(k // 2)
        if waiting:
            collect(waiting.pop(0))
        waiting.append(k)
    for k in rest:
        produce(k // 2)
        if waiting:
            collect(waiting.pop(0))
    for k in rest:
        collect(k)

    for k in range(1, n):
        b = low(k)
        for p in range(pieces):
            ag_copy(k - b, b, p).wait_send()
            if b > 1 or p == 0:
                rs_copy(k, p).wait_send()
    d_copy.wait()


def fused(n, act, target, weights, delta):
    tokens, feats = act.shape
    rows, width = weights.shape
    dma = pltpu.SemaphoreType.DMA
    bf, f32 = jnp.bfloat16, jnp.float32
    return pl.pallas_call(
        functools.partial(kernel, n, PIECES, feats ** (-0.5)),
        out_shape=(
            jax.ShapeDtypeStruct((rows, width), f32),
            jax.ShapeDtypeStruct((rows, width), f32),
        ),
        in_specs=[pl.BlockSpec(memory_space=pl.ANY)] * 4,
        out_specs=(pl.BlockSpec(memory_space=pltpu.VMEM), pl.BlockSpec(memory_space=pl.ANY)),
        scratch_shapes=[
            pltpu.VMEM((rows, width), f32),
            pltpu.VMEM((n // 2, 2 * rows, width), bf),
            pltpu.VMEM((n // 2, tokens, 2 * rows), bf),
            pltpu.VMEM((n // 2, 2 * rows, tokens), bf),
            pltpu.VMEM((tokens, width), f32),
            pltpu.VMEM((tokens, width), bf),
            pltpu.VMEM((tokens, width), bf),
            pltpu.VMEM((n // 2, 2 * rows, width), f32),
            pltpu.VMEM((n, rows, width), bf),
            pltpu.VMEM((n, rows, width), bf),
            dma, dma((n // 2,)), dma,
            dma((n, PIECES)), dma((n, PIECES)), dma((n, PIECES)), dma((n, PIECES)),
            dma, dma,
        ],
        compiler_params=pltpu.CompilerParams(collective_id=0, has_side_effects=True),
    )(act, target, weights, delta)


def plain_grad(act, target, low_rows, in_scale):
    whole = lax.all_gather(low_rows, "fsdp", axis=0, tiled=True)
    predicted = jnp.dot(act, whole, preferred_element_type=jnp.float32) * in_scale
    resid = (predicted - target.astype(jnp.float32)).astype(jnp.bfloat16)
    part = lax.dot_general(act, resid, (((0,), (0,)), ((), ())), preferred_element_type=jnp.float32)
    return lax.psum_scatter(part, "fsdp", scatter_dimension=0, tiled=True)


def plain_outer(outer_delta, anchor, outer_mom):
    groups = lax.axis_size("replica")
    block = anchor.shape[1] // groups
    blocks = lax.all_to_all(outer_delta, "replica", split_axis=2, concat_axis=0, tiled=True)
    mean = jnp.sum(blocks, axis=0) / groups
    offset = lax.axis_index("replica") * block
    mom = 0.9 * lax.dynamic_slice_in_dim(outer_mom, offset, block, 1) + mean
    anchor = lax.dynamic_slice_in_dim(anchor, offset, block, 1) - 0.7 * (mean + 0.9 * mom)
    return (
        lax.all_gather(anchor, "replica", axis=1, tiled=True),
        lax.all_gather(mom, "replica", axis=1, tiled=True),
    )


def body(act, target, weights, inner_m, inner_v, outer_delta, anchor, outer_mom):
    n = lax.axis_size("fsdp")
    groups = lax.axis_size("replica")
    micro, tok, feats = act.shape[1:]
    width = weights.shape[2]
    in_scale = feats ** (-0.5)
    flat_act = act[0].reshape(micro * tok, feats)
    flat_target = target[0].reshape(micro * tok, width)
    fits = groups == 2 and 4 <= n <= LIMIT and n & (n - 1) == 0
    if fits:
        grad_rows, peer = fused(n, flat_act, flat_target, weights[0], outer_delta[0])
        mean = (outer_delta[0] + peer) / groups
        new_mom = 0.9 * outer_mom + mean
        new_anchor = anchor - 0.7 * (mean + 0.9 * new_mom)
    else:
        grad_rows = plain_grad(flat_act, flat_target, weights[0].astype(jnp.bfloat16), in_scale)
        new_anchor, new_mom = plain_outer(outer_delta, anchor, outer_mom)
    grad = grad_rows * (in_scale / (micro * tok * n))
    moment = 0.9 * inner_m[0] + 0.1 * grad
    second = 0.95 * inner_v[0] + 0.05 * grad * grad
    trained = weights[0] - 0.3 * moment / (jnp.sqrt(second) + 1e-08)
    mixed = 0.5 * trained + 0.5 * new_anchor
    return (mixed[None], moment[None], second[None], new_anchor, new_mom)


def solution(mesh):
    split = P("replica", None, "fsdp", None)
    both = P("replica", "fsdp", None)
    one = P("fsdp", None)
    return jax.shard_map(
        body,
        mesh=mesh,
        in_specs=(split, split, both, both, both, both, one, one),
        out_specs=(both, both, both, one, one),
        check_vma=False,
    )
```

time: 147 us -> 44.2 us (0.30)
  waiting for transfers between devices: 98.8 us -> 0 us
  Pallas kernels: 0 us -> 41.1 us
  between operations: 14.2 us -> 0.74 us
  blocking collectives: 11.3 us -> 0 us
  local copies, waits for them, and re-layouts: 8.42 us -> 0.03 us
  matrix products: 8.09 us -> 0 us
  starting transfers between devices: 3.53 us -> 0 us
    reduce_scatter x1 -> x0, waiting for transfers between devices: 48 us -> none  [body(): lax.psum_scatter(lax.dot_general(flat_act, resid, (((0,), (0,)), ((), ())...]
    all_gather x1 -> x0, waiting for transfers between devices: 45.4 us -> none  [body(): lax.all_gather(shard_low, 'fsdp', axis=0, tiled=True)]
    pallas_call x0 -> x1, Pallas kernels: none -> 41.1 us  [fused(): pl.pallas_call(functools.partial(kernel, n, PIECES, feats ** (-0.5)), out...]
    all_gather x2 -> x0, blocking collectives: 11.3 us -> none  [the longest x1 5.64 us: body(): lax.all_gather(anchor_next, 'replica', axis=1, tiled=True)]
    unnamed x27 -> x12, local copies, waits for them, and re-layouts: 8.39 us -> 0.03 us
    dot_general x3 -> x0, matrix products: 8.09 us -> none  [the longest x2 4.26 us: add_rows(): return jnp.dot(inputs, piece, preferred_element_type=jnp.float32)]
    all_to_all x1 -> x0, waiting for transfers between devices: 5.3 us -> none  [body(): lax.all_to_all(outer_delta, 'replica', split_axis=2, concat_axis=0, tiled...]
    all_to_all x1 -> x0, starting transfers between devices: 3.45 us -> none  [body(): lax.all_to_all(outer_delta, 'replica', split_axis=2, concat_axis=0, tiled...]
  transfers between devices with their start and end apart: 3 -> 0, of which waited for: 3 -> 0; matrix products, arithmetic and copies ran while one was open for 2% -> 0% of each run, Pallas kernels for 0% -> 0%
where the time goes in v1:
time: 44.2 us; the launch traced here: 44.1 us
  Pallas kernels  41.1 us (93%)
  other arithmetic  2.2 us (5%)
  between operations  0.74 us (2%)
    pallas_call x1, Pallas kernels, fused(): pl.pallas_call(functools.partial(kernel, n, PIECES, feats ** (-0.5)), out...  41.1 us
    broadcast_in_dim x1, other arithmetic, body(): return (mixed[None], moment[None], second[None], new_anchor, new_mom)  2.2 us

profile of v1, /device:TPU:0, one launch (start us, length us, event | category | flops | bytes accessed | tf_op | source)
XLA Modules:
  0.0 44.1 jit_solution(3471764880262981797)
XLA Ops:
  0.6 0.0 copy-start.1
  0.6 0.0 copy-start
  0.7 0.0 copy-start.5
  0.7 0.0 copy-start.4
  0.7 0.0 copy-start.3
  0.7 0.0 copy-start.2
  0.7 41.1 %shard_map.119 = (f32[128,512]{1,0:T(8,128)}, f32[128,512]{1,0:T(8,128)}) custom-call(bf16[768,2048]{1,0:T(8,128)(2,1)} %bitcast.27, bf16[768,512]{1,0:T(8,128)(2,1)} %bitcast.30, f32[128,512]{1,0:T(8,128)} %bitcast.28, f32[128,512]{1,0:T(8,128)} %bitcast.29), custom_call_target="tpu_custom_call" | custom-call | tf_op jit(solution)/shard_map/pallas_call | solution.py:225
  41.8 0.0 copy-done.1
  41.8 0.0 copy-done
  41.8 0.0 copy-done.5
  41.9 0.0 copy-done.4
  41.9 0.0 copy-done.3
  41.9 0.0 copy-done.2
  41.9 2.2 %multiply_bitcast_fusion = (f32[1,128,512]{2,1,0:T(8,128)}, f32[128,512]{1,0:T(8,128)}, f32[128,512]{1,0:T(8,128)}, f32[1,128,512]{2,1,0:T(8,128)}, f32[1,128,512]{2,1,0:T(8,128)}) fusion(f32[128,512]{1,0:T(8,128)} %get-tuple-element.7, f32[1,128,512]{2,1,0:T(8,128)S(1)} %copy-done.2, f32[1,128,512]{2,1,0:T(8,128)S(1)} %copy-done.3, ...), kind=kLoop, calls=%fused_computation.2 | loop fusion | flops 1441792 | bytes 3407872 | tf_op jit(solution)/shard_map/broadcast_in_dim | solution.py:296
Async XLA Ops:
  0.6 41.2 %copy-start.1 = (f32[1,128,512]{2,1,0:T(8,128)S(1)}, f32[1,128,512]{2,1,0:T(8,128)}, u32[]{:S(2)}) copy-start(f32[1,128,512]{2,1,0:T(8,128)} %param.13) | copy-start | bytes 786436
  0.6 41.2 %copy-start = (f32[1,128,512]{2,1,0:T(8,128)S(1)}, f32[1,128,512]{2,1,0:T(8,128)}, u32[]{:S(2)}) copy-start(f32[1,128,512]{2,1,0:T(8,128)} %param.10) | copy-start | bytes 786436
  0.7 41.2 %copy-start.5 = (f32[128,512]{1,0:T(8,128)S(1)}, f32[128,512]{1,0:T(8,128)}, u32[]{:S(2)}) copy-start(f32[128,512]{1,0:T(8,128)} %param.15) | copy-start | bytes 786436
  0.7 41.2 %copy-start.4 = (f32[128,512]{1,0:T(8,128)S(1)}, f32[128,512]{1,0:T(8,128)}, u32[]{:S(2)}) copy-start(f32[128,512]{1,0:T(8,128)} %param.14) | copy-start | bytes 786436
  0.7 41.2 %copy-start.3 = (f32[1,128,512]{2,1,0:T(8,128)S(1)}, f32[1,128,512]{2,1,0:T(8,128)}, u32[]{:S(2)}) copy-start(f32[1,128,512]{2,1,0:T(8,128)} %param.12) | copy-start | bytes 786436
  0.7 41.2 %copy-start.2 = (f32[1,128,512]{2,1,0:T(8,128)S(1)}, f32[1,128,512]{2,1,0:T(8,128)}, u32[]{:S(2)}) copy-start(f32[1,128,512]{2,1,0:T(8,128)} %param.11) | copy-start | bytes 786436

commit v2 on v1

--- a/solution.py
+++ b/solution.py
@@ -88,8 +88,8 @@
             device_id_type=MESH,
         )
 
-    for b in reversed(bits):
-        for p in range(pieces):
+    for p in range(pieces):
+        for b in reversed(bits):
             ag_copy(0, b, p).start()
     d_copy = pltpu.make_async_remote_copy(
         src_ref=delta, dst_ref=peer_out, send_sem=d_send, recv_sem=d_recv,
@@ -225,11 +225,11 @@
     return pl.pallas_call(
         functools.partial(kernel, n, PIECES, feats ** (-0.5)),
         out_shape=(
-            jax.ShapeDtypeStruct((rows, width), f32),
-            jax.ShapeDtypeStruct((rows, width), f32),
+            pltpu.VMEM((rows, width), f32),
+            pltpu.VMEM((rows, width), f32),
         ),
         in_specs=[pl.BlockSpec(memory_space=pl.ANY)] * 4,
-        out_specs=(pl.BlockSpec(memory_space=pltpu.VMEM), pl.BlockSpec(memory_space=pl.ANY)),
+        out_specs=(pl.BlockSpec(memory_space=pltpu.VMEM), pl.BlockSpec(memory_space=pltpu.VMEM)),
         scratch_shapes=[
             pltpu.VMEM((rows, width), f32),
             pltpu.VMEM((n // 2, 2 * rows, width), bf),

time: 44.2 us -> 42.2 us (0.955)
  other arithmetic: 2.2 us -> 1.18 us
  Pallas kernels: 41.1 us -> 40.1 us
    pallas_call x1, Pallas kernels: 41.1 us -> 40.1 us  [fused(): pl.pallas_call(functools.partial(kernel, n, PIECES, feats ** (-0.5)), out...]
    broadcast_in_dim x1, other arithmetic: 2.2 us -> 1.18 us  [body(): return (mixed[None], moment[None], second[None], new_anchor, new_mom)]
where the time goes in v2:
time: 42.2 us; the launch traced here: 42 us
  Pallas kernels  40.1 us (95%)
  other arithmetic  1.18 us (3%)
  between operations  0.74 us (2%)
    pallas_call x1, Pallas kernels, fused(): pl.pallas_call(functools.partial(kernel, n, PIECES, feats ** (-0.5)), out...  40.1 us
    broadcast_in_dim x1, other arithmetic, body(): return (mixed[None], moment[None], second[None], new_anchor, new_mom)  1.18 us

profile of v2, /device:TPU:0, one launch (start us, length us, event | category | flops | bytes accessed | tf_op | source)
XLA Modules:
  0.0 42.0 jit_solution(3345512489025822973)
XLA Ops:
  0.6 0.0 copy-start.1
  0.6 0.0 copy-start
  0.7 0.0 copy-start.5
  0.7 0.0 copy-start.4
  0.7 0.0 copy-start.3
  0.7 0.0 copy-start.2
  0.7 40.1 %shard_map.119 = (f32[128,512]{1,0:T(8,128)S(1)}, f32[128,512]{1,0:T(8,128)S(1)}) custom-call(bf16[768,2048]{1,0:T(8,128)(2,1)} %bitcast.27, bf16[768,512]{1,0:T(8,128)(2,1)} %bitcast.30, f32[128,512]{1,0:T(8,128)} %bitcast.28, f32[128,512]{1,0:T(8,128)} %bitcast.29), custom_call_target="tpu_custom_call" | custom-call | tf_op jit(solution)/shard_map/pallas_call | solution.py:225
  40.8 0.0 copy-done.1
  40.8 0.0 copy-done
  40.8 0.0 copy-done.5
  40.8 0.0 copy-done.4
  40.8 0.0 copy-done.3
  40.8 0.0 copy-done.2
  40.8 1.2 %multiply_bitcast_fusion = (f32[1,128,512]{2,1,0:T(8,128)}, f32[128,512]{1,0:T(8,128)}, f32[128,512]{1,0:T(8,128)}, f32[1,128,512]{2,1,0:T(8,128)}, f32[1,128,512]{2,1,0:T(8,128)}) fusion(f32[128,512]{1,0:T(8,128)S(1)} %get-tuple-element.7, f32[1,128,512]{2,1,0:T(8,128)S(1)} %copy-done.2, f32[1,128,512]{2,1,0:T(8,128)S(1)} %copy-done.3, ...), kind=kLoop, calls=%fused_computation.2 | loop fusion | flops 1441792 | bytes 3407872 | tf_op jit(solution)/shard_map/broadcast_in_dim | solution.py:296
Async XLA Ops:
  0.6 40.2 %copy-start.1 = (f32[1,128,512]{2,1,0:T(8,128)S(1)}, f32[1,128,512]{2,1,0:T(8,128)}, u32[]{:S(2)}) copy-start(f32[1,128,512]{2,1,0:T(8,128)} %param.13) | copy-start | bytes 786436
  0.6 40.2 %copy-start = (f32[1,128,512]{2,1,0:T(8,128)S(1)}, f32[1,128,512]{2,1,0:T(8,128)}, u32[]{:S(2)}) copy-start(f32[1,128,512]{2,1,0:T(8,128)} %param.10) | copy-start | bytes 786436
  0.7 40.2 %copy-start.5 = (f32[128,512]{1,0:T(8,128)S(1)}, f32[128,512]{1,0:T(8,128)}, u32[]{:S(2)}) copy-start(f32[128,512]{1,0:T(8,128)} %param.15) | copy-start | bytes 786436
  0.7 40.2 %copy-start.4 = (f32[128,512]{1,0:T(8,128)S(1)}, f32[128,512]{1,0:T(8,128)}, u32[]{:S(2)}) copy-start(f32[128,512]{1,0:T(8,128)} %param.14) | copy-start | bytes 786436
  0.7 40.2 %copy-start.3 = (f32[1,128,512]{2,1,0:T(8,128)S(1)}, f32[1,128,512]{2,1,0:T(8,128)}, u32[]{:S(2)}) copy-start(f32[1,128,512]{2,1,0:T(8,128)} %param.12) | copy-start | bytes 786436
  0.7 40.2 %copy-start.2 = (f32[1,128,512]{2,1,0:T(8,128)S(1)}, f32[1,128,512]{2,1,0:T(8,128)}, u32[]{:S(2)}) copy-start(f32[1,128,512]{2,1,0:T(8,128)} %param.11) | copy-start | bytes 786436
